TPU v7x, 32 devices: a whole 2x2x4 slice. The times are simulated.
32 devices in a mesh: gz: 2 (over core), row: 4 (over y, x), col: 4 (over z).
Axes of the slice: x: 2, y: 2, z: 4, core: 2. Of those that a mesh axis runs over, the one named last changes fastest.
Arguments:
- right_sides: float32 [32, 4, 16, 256], P(('gz', 'row', 'col')), may hold values from -6 to 6
- lower_inverse: bfloat16 [32, 4, 256, 256], P(('gz', 'row', 'col')), may hold values from -0.375 to 0.375
- upper_inverse: bfloat16 [32, 4, 256, 256], P(('gz', 'row', 'col')), may hold values from -0.375 to 0.375
- lower_blocks: bfloat16 [32, 4, 2, 256, 256], P(('gz', 'row', 'col')), may hold values from -0.125 to 0.125
- upper_blocks: bfloat16 [32, 4, 2, 256, 256], P(('gz', 'row', 'col')), may hold values from -0.125 to 0.125
- node_widths: int32 [32, 4], P(('gz', 'row', 'col')), may hold values from 128 to 256, as said below
- far_levels: int32 [32, 4], P(('gz', 'row', 'col')), may hold values from 0 to 5, as said below
- owner_level: int32 [32], replicated, may hold values from 0 to 5, as said below
Outputs:
- solution: float32 [32, 4, 16, 256], P(('gz', 'row', 'col'))
Inputs may be any that keep to these rules, and one draw needn't show every extreme that they name: Columns c >= node_widths of a supernode are padding; every device holds a supernode with all 256 columns. `far_levels`: between 2 and 5 where the supernode has two or more ancestors, but never past the root; 1 where it has one; 0 for the root and for the slot of the device that owns no separator. `owner_level`: every separator of level u is owned by exactly one device of its group (the devices t with the same t // 2**u); one device owns none and holds 0.
All inputs are finite; a program needn't handle non-finite values.
Results may differ from a plain program's by a relative error of at most 0.018.
Values may be sent and summed in bfloat16 or wider, within the bound.
A program may use at most 64 MiB of HBM per device.

v0:
```python
import jax
import jax.numpy as jnp
from jax import lax
from jax.sharding import PartitionSpec as P

W = 256
RHS = 16
NB = 2
LOCAL_LEVELS = 2
LOCAL_COUNT = 3


def level_start(height):
    return 2**LOCAL_LEVELS - 2 ** (LOCAL_LEVELS - height)


def apply_blocks(vectors, blocks):
    return jnp.einsum("snrk,snak->snra", vectors, blocks, preferred_element_type=jnp.float32)


def apply_single(vectors, blocks):
    return jnp.einsum("srk,sak->sra", vectors, blocks, preferred_element_type=jnp.float32)


def forward_local(right_sides, lower_inverse, lower_blocks, padding, far_levels, upper_levels):
    batch_size = right_sides.shape[0]
    pending = jnp.zeros((batch_size, LOCAL_COUNT, RHS, W), jnp.float32)
    upper_pending = jnp.zeros((batch_size, upper_levels, RHS, W), jnp.float32)
    solved = []
    for height in range(LOCAL_LEVELS):
        offset = level_start(height)
        amount = 2 ** (LOCAL_LEVELS - 1 - height)
        residue = (
            right_sides[:, offset : offset + amount] - pending[:, offset : offset + amount]
        ).astype(jnp.bfloat16)
        solved_now = padding[:, offset : offset + amount] * apply_blocks(
            residue, lower_inverse[:, offset : offset + amount]
        )
        solved.append(solved_now)
        rounded = solved_now.astype(jnp.bfloat16)
        for block_id in range(NB):
            product = apply_blocks(rounded, lower_blocks[:, offset : offset + amount, block_id])
            for distance in range(1, upper_levels + 1):
                if block_id == 0 and distance > 1:
                    continue
                if block_id == 0:
                    chosen = product
                else:
                    matches = far_levels[:, offset : offset + amount] == distance
                    chosen = jnp.where(matches[:, :, None, None], product, 0.0)
                target = height + distance
                if target < LOCAL_LEVELS:
                    target_count = amount // 2**distance
                    folded = chosen.reshape(batch_size, target_count, 2**distance, RHS, W).sum(
                        axis=2
                    )
                    begin_at = level_start(target)
                    pending = pending.at[:, begin_at : begin_at + target_count].add(folded)
                else:
                    upper_pending = upper_pending.at[:, target - LOCAL_LEVELS].add(
                        chosen.sum(axis=1)
                    )
    return (jnp.concatenate(solved, axis=1), upper_pending)


def backward_local(forward, upper_inverse, upper_blocks, padding, far_levels, upper_known):
    upper_levels = upper_known.shape[1]
    solutions = [None] * LOCAL_LEVELS
    for height in reversed(range(LOCAL_LEVELS)):
        offset = level_start(height)
        amount = 2 ** (LOCAL_LEVELS - 1 - height)
        residue = forward[:, offset : offset + amount]
        for block_id in range(NB):
            operand = jnp.zeros(residue.shape, jnp.float32)
            for distance in range(1, upper_levels + 1):
                if block_id == 0 and distance > 1:
                    continue
                target = height + distance
                if target < LOCAL_LEVELS:
                    known_part = jnp.repeat(solutions[target], 2**distance, axis=1)
                else:
                    known_part = jnp.broadcast_to(
                        upper_known[:, target - LOCAL_LEVELS][:, None], residue.shape
                    )
                if block_id == 0:
                    operand = known_part
                else:
                    matches = far_levels[:, offset : offset + amount] == distance
                    operand = operand + jnp.where(matches[:, :, None, None], known_part, 0.0)
            residue = residue - apply_blocks(
                operand.astype(jnp.bfloat16), upper_blocks[:, offset : offset + amount, block_id]
            )
        solutions[height] = padding[:, offset : offset + amount] * apply_blocks(
            residue.astype(jnp.bfloat16), upper_inverse[:, offset : offset + amount]
        )
    return jnp.concatenate(solutions, axis=1)


def spread_slots(partial_value, slot_count, slot_at):
    chosen = (jnp.arange(slot_count, dtype=jnp.int32) == slot_at)[:, None, None]
    return jnp.where(chosen, partial_value, 0.0)


def group_total(partial_value, height, layout, places):
    col_levels, grid_levels, col_span, grid_span, total_span = layout
    if height <= col_levels:
        slot_at = places[0] // 2**height
        summed = lax.psum(
            spread_slots(partial_value, col_span // 2**height, slot_at).astype(jnp.bfloat16), "col"
        ).astype(jnp.float32)
    elif height <= grid_levels:
        slot_at = places[1] // 2**height
        summed = lax.psum(
            spread_slots(partial_value, grid_span // 2**height, slot_at), ("row", "col")
        )
    else:
        slot_at = places[2] // 2**height
        summed = lax.psum(
            spread_slots(partial_value, total_span // 2**height, slot_at), ("gz", "row", "col")
        )
    return lax.dynamic_index_in_dim(summed, slot_at, 0, keepdims=True)


def group_share(partial_value, height, layout, places):
    col_levels, grid_levels, col_span, grid_span, total_span = layout
    if height <= col_levels:
        slot_at = places[0] // 2**height
        summed = lax.psum(
            spread_slots(partial_value, col_span // 2**height, slot_at).astype(jnp.bfloat16), "col"
        ).astype(jnp.float32)
    elif height <= grid_levels:
        slot_at = places[1] // 2**height
        summed = lax.psum(
            spread_slots(partial_value, grid_span // 2**height, slot_at), ("row", "col")
        )
    else:
        slot_at = places[2] // 2**height
        summed = lax.psum(
            spread_slots(partial_value, total_span // 2**height, slot_at), ("gz", "row", "col")
        )
    return lax.dynamic_index_in_dim(summed, slot_at, 0, keepdims=True)


def local(
    right_sides,
    lower_inverse,
    upper_inverse,
    lower_blocks,
    upper_blocks,
    node_widths,
    far_levels,
    owner_level,
):
    col_span = lax.axis_size("col")
    row_span = lax.axis_size("row")
    layer_span = lax.axis_size("gz")
    col_levels = col_span.bit_length() - 1
    grid_levels = col_levels + row_span.bit_length() - 1
    upper_levels = grid_levels + layer_span.bit_length() - 1
    col_place = lax.axis_index("col")
    grid_place = lax.axis_index("row") * col_span + col_place
    device = lax.axis_index("gz") * row_span * col_span + grid_place
    layout = (
        col_levels,
        grid_levels,
        col_span,
        row_span * col_span,
        layer_span * row_span * col_span,
    )
    places = (col_place, grid_place, device)
    columns = jnp.arange(W, dtype=jnp.int32)
    padding = (columns[None, None, None, :] < node_widths[:, :, None, None]).astype(jnp.float32)
    forward_nodes, upper_pending = forward_local(
        right_sides[:, :LOCAL_COUNT],
        lower_inverse[:, :LOCAL_COUNT],
        lower_blocks[:, :LOCAL_COUNT],
        padding[:, :LOCAL_COUNT],
        far_levels[:, :LOCAL_COUNT],
        upper_levels,
    )
    own_rights = right_sides[:, LOCAL_COUNT]
    own_padding = padding[:, LOCAL_COUNT]
    own_far = far_levels[:, LOCAL_COUNT]
    my_level = lax.dynamic_index_in_dim(owner_level, device, 0, keepdims=False)
    own_forward = jnp.zeros((1, RHS, W), jnp.float32)
    for height in range(1, upper_levels + 1):
        gathered = group_total(upper_pending[:, height - 1], height, layout, places)
        owner_here = my_level == height
        residue = (own_rights - gathered).astype(jnp.bfloat16)
        solved_now = jnp.where(
            owner_here, own_padding * apply_single(residue, lower_inverse[:, LOCAL_COUNT]), 0.0
        )
        own_forward = own_forward + solved_now
        rounded = solved_now.astype(jnp.bfloat16)
        for block_id in range(NB):
            product = apply_single(rounded, lower_blocks[:, LOCAL_COUNT, block_id])
            for distance in range(1, upper_levels + 1):
                if block_id == 0 and distance > 1:
                    continue
                target = height + distance
                if target > upper_levels:
                    continue
                if block_id == 0:
                    chosen = product
                else:
                    chosen = jnp.where((own_far == distance)[:, None, None], product, 0.0)
                upper_pending = upper_pending.at[:, target - 1].add(chosen)
    upper_known = jnp.zeros((1, upper_levels, RHS, W), jnp.float32)
    own_solution = jnp.zeros((1, RHS, W), jnp.float32)
    for height in range(upper_levels, 0, -1):
        owner_here = my_level == height
        residue = own_forward
        for block_id in range(NB):
            operand = jnp.zeros((1, RHS, W), jnp.float32)
            for distance in range(1, upper_levels + 1):
                if block_id == 0 and distance > 1:
                    continue
                target = height + distance
                if target > upper_levels:
                    continue
                known_part = upper_known[:, target - 1]
                if block_id == 0:
                    operand = known_part
                else:
                    operand = operand + jnp.where(
                        (own_far == distance)[:, None, None], known_part, 0.0
                    )
            residue = residue - apply_single(
                operand.astype(jnp.bfloat16), upper_blocks[:, LOCAL_COUNT, block_id]
            )
        solved_now = jnp.where(
            owner_here,
            own_padding * apply_single(residue.astype(jnp.bfloat16), upper_inverse[:, LOCAL_COUNT]),
            0.0,
        )
        own_solution = own_solution + solved_now
        shared = group_share(solved_now, height, layout, places)
        upper_known = upper_known.at[:, height - 1].set(shared)
    local_solution = backward_local(
        forward_nodes,
        upper_inverse[:, :LOCAL_COUNT],
        upper_blocks[:, :LOCAL_COUNT],
        padding[:, :LOCAL_COUNT],
        far_levels[:, :LOCAL_COUNT],
        upper_known,
    )
    return jnp.concatenate([local_solution, own_solution[:, None]], axis=1)


def solution(mesh):
    return jax.shard_map(
        local,
        mesh=mesh,
        in_specs=(
            P(("gz", "row", "col"), None, None, None),
            P(("gz", "row", "col"), None, None, None),
            P(("gz", "row", "col"), None, None, None),
            P(("gz", "row", "col"), None, None, None, None),
            P(("gz", "row", "col"), None, None, None, None),
            P(("gz", "row", "col"), None),
            P(("gz", "row", "col"), None),
            P(),
        ),
        out_specs=P(("gz", "row", "col"), None, None, None),
        check_vma=False,
    )
```

profile of v0, /device:TPU:0, one launch (start us, length us, event | category | flops | bytes accessed | tf_op | source)
XLA Modules:
  0.0 453.6 jit_solution(13407759819667578866)
XLA Ops:
  0.0 0.7 compare_bitcast_fusion.3
  0.8 0.7 fusion.307
  1.5 1.1 convolution_multiply_fusion.1
  2.6 1.2 select_reduce_fusion.4
  3.9 1.4 convolution_multiply_fusion.13
  5.5 0.7 copy-done.5
  6.1 0.6 fusion.324
  10.2 20.5 %psum.70 = bf16[2,16,256]{2,1,0:T(8,128)(2,1)S(1)} all-reduce(bf16[2,16,256]{2,1,0:T(8,128)(2,1)S(1)} %select_convert_fusion.1), channel_id=1, replica_groups=mesh['gz'=2,'row'=4,'col'=4] {'col'}, use_global_device_ids=true, to_apply=%region_5.6 | all-reduce | flops 8192 | bytes 32768 | tf_op jit(solution)/shard_map/psum | solution.py:108
  30.7 0.7 copy-done.6
  31.4 0.6 dynamic_slice.24
  32.8 0.2 fusion.22
  35.9 8.5 %psum.71 = bf16[1,16,256]{2,1,0:T(8,128)(2,1)S(1)} all-reduce(bf16[1,16,256]{2,1,0:T(8,128)(2,1)S(1)} %fusion.218), channel_id=1, replica_groups=mesh['gz'=2,'row'=4,'col'=4] {'col'}, use_global_device_ids=true, to_apply=%region_6.7 | all-reduce | flops 4096 | bytes 16384 | tf_op jit(solution)/shard_map/psum | solution.py:108
  45.2 0.2 fusion.20
  45.8 75.8 %psum.72 = f32[2,16,256]{2,1,0:T(8,128)S(1)} all-reduce(f32[2,16,256]{2,1,0:T(8,128)S(1)} %broadcast_select_fusion.1), channel_id=1, replica_groups=mesh['gz'=2,'row'=4,'col'=4] {'row','col'}, use_global_device_ids=true, to_apply=%region_7.8 | all-reduce | flops 8192 | bytes 65536 | tf_op jit(solution)/shard_map/psum | solution.py:113
  122.6 0.2 fusion.18
  122.8 72.1 %psum.73 = f32[1,16,256]{2,1,0:T(8,128)S(1)} all-reduce(f32[1,16,256]{2,1,0:T(8,128)S(1)} %fusion.18), channel_id=1, replica_groups=mesh['gz'=2,'row'=4,'col'=4] {'row','col'}, use_global_device_ids=true, to_apply=%region_8.9 | all-reduce | flops 4096 | bytes 32768 | tf_op jit(solution)/shard_map/psum | solution.py:113
  195.7 0.2 fusion.13
  195.9 0.2 fusion.12
  196.0 36.9 %psum.74 = f32[1,16,256]{2,1,0:T(8,128)S(1)} all-reduce(f32[1,16,256]{2,1,0:T(8,128)S(1)} %fusion.12), channel_id=1, replica_groups=mesh['gz'=2,'row'=4,'col'=4] {'gz','row','col'}, use_global_device_ids=true, to_apply=%region_9.10 | all-reduce | flops 4096 | bytes 32768 | tf_op jit(solution)/shard_map/psum | solution.py:118
  233.9 0.3 fusion.6
  234.3 41.4 %psum.75 = f32[1,16,256]{2,1,0:T(8,128)S(1)} all-reduce(f32[1,16,256]{2,1,0:T(8,128)S(1)} %select_bitcast_fusion.1), channel_id=1, replica_groups=mesh['gz'=2,'row'=4,'col'=4] {'gz','row','col'}, use_global_device_ids=true, to_apply=%region_10.11 | all-reduce | flops 4096 | bytes 32768 | tf_op jit(solution)/shard_map/psum | solution.py:138
  275.9 0.3 fusion.5
  276.2 76.1 %psum.76 = f32[1,16,256]{2,1,0:T(8,128)S(1)} all-reduce(f32[1,16,256]{2,1,0:T(8,128)S(1)} %select_bitcast_fusion), channel_id=1, replica_groups=mesh['gz'=2,'row'=4,'col'=4] {'row','col'}, use_global_device_ids=true, to_apply=%region_11.12 | all-reduce | flops 4096 | bytes 32768 | tf_op jit(solution)/shard_map/psum | solution.py:133
  352.5 0.3 fusion.4
  352.9 72.1 %psum.77 = f32[2,16,256]{2,1,0:T(8,128)S(1)} all-reduce(f32[2,16,256]{2,1,0:T(8,128)S(1)} %broadcast_select_fusion), channel_id=1, replica_groups=mesh['gz'=2,'row'=4,'col'=4] {'row','col'}, use_global_device_ids=true, to_apply=%region_12.13 | all-reduce | flops 8192 | bytes 65536 | tf_op jit(solution)/shard_map/psum | solution.py:133
  425.1 0.3 fusion.3
  425.4 8.5 %psum.78 = bf16[1,16,256]{2,1,0:T(8,128)(2,1)S(1)} all-reduce(bf16[1,16,256]{2,1,0:T(8,128)(2,1)S(1)} %fusion.201), channel_id=1, replica_groups=mesh['gz'=2,'row'=4,'col'=4] {'col'}, use_global_device_ids=true, to_apply=%region_13.14 | all-reduce | flops 4096 | bytes 16384 | tf_op jit(solution)/shard_map/psum | solution.py:128
  434.1 0.3 fusion.2
  434.5 17.4 %psum.79 = bf16[2,16,256]{2,1,0:T(8,128)(2,1)S(1)} all-reduce(bf16[2,16,256]{2,1,0:T(8,128)(2,1)S(1)} %select_convert_fusion), channel_id=1, replica_groups=mesh['gz'=2,'row'=4,'col'=4] {'col'}, use_global_device_ids=true, to_apply=%region_14.15 | all-reduce | flops 8192 | bytes 32768 | tf_op jit(solution)/shard_map/psum | solution.py:128
  452.1 0.3 fusion.325
  452.6 0.3 fusion
  453.0 0.6 pad_maximum_fusion
  (65 shorter events, 3.3 us)
Async XLA Ops:
  0.0 5.3 %copy-start.1 = (bf16[1,4,2,256,256]{4,3,2,1,0:T(8,128)(2,1)S(1)}, bf16[1,4,2,256,256]{4,3,2,1,0:T(8,128)(2,1)}, u32[]{:S(2)}) copy-start(bf16[1,4,2,256,256]{4,3,2,1,0:T(8,128)(2,1)} %param.73) | copy-start | bytes 3145732
  3.9 28.8 %copy-start.2 = (bf16[1,4,256,256]{3,2,1,0:T(8,128)(2,1)S(1)}, bf16[1,4,256,256]{3,2,1,0:T(8,128)(2,1)}, u32[]{:S(2)}) copy-start(bf16[1,4,256,256]{3,2,1,0:T(8,128)(2,1)} %param.71) | copy-start | bytes 1572868
  5.5 0.7 copy-start.5
  10.1 22.6 %copy-start.4 = (f32[1,4,16,256]{3,2,1,0:T(8,128)S(1)}, f32[1,4,16,256]{3,2,1,0:T(8,128)}, u32[]{:S(2)}) copy-start(f32[1,4,16,256]{3,2,1,0:T(8,128)} %param.70) | copy-start | bytes 196612
  30.7 0.7 copy-start.6
  45.4 188.3 %copy-start = (bf16[1,4,2,256,256]{4,3,2,1,0:T(8,128)(2,1)S(1)}, bf16[1,4,2,256,256]{4,3,2,1,0:T(8,128)(2,1)}, u32[]{:S(2)}) copy-start(bf16[1,4,2,256,256]{4,3,2,1,0:T(8,128)(2,1)} %param.74) | copy-start | bytes 3145732
  195.5 38.4 %copy-start.3 = (bf16[1,4,256,256]{3,2,1,0:T(8,128)(2,1)S(1)}, bf16[1,4,256,256]{3,2,1,0:T(8,128)(2,1)}, u32[]{:S(2)}) copy-start(bf16[1,4,256,256]{3,2,1,0:T(8,128)(2,1)} %param.72) | copy-start | bytes 1572868
where the time goes:
time: 454 us
  blocking collectives  429 us (94%)
  matrix products  9.61 us (2%)
  between operations  9.28 us (2%)
    psum x2, blocking collectives, group_share(): lax.psum(spread_slots(partial_value, grid_span // 2 ** height, slot_at),...  148 us
    psum x2, blocking collectives, group_total(): lax.psum(spread_slots(partial_value, grid_span // 2 ** height, slot_at),...  148 us
    psum x1, blocking collectives, group_share(): lax.psum(spread_slots(partial_value, total_span // 2 ** height, slot_at),...  41.4 us
    psum x1, blocking collectives, group_total(): lax.psum(spread_slots(partial_value, total_span // 2 ** height, slot_at),...  36.9 us
    psum x2, blocking collectives, group_total(): lax.psum(spread_slots(partial_value, col_span // 2 ** height, slot_at).as...  29 us
    psum x2, blocking collectives, group_share(): lax.psum(spread_slots(partial_value, col_span // 2 ** height, slot_at).as...  25.9 us

commit v1 on v0

--- a/solution.py
+++ b/solution.py
@@ -8,6 +8,11 @@
 NB = 2
 LOCAL_LEVELS = 2
 LOCAL_COUNT = 3
+
+
+def by_each_axis(value, axis_one, axis_two):
+    inner = lax.psum(value, axis_one)
+    return lax.psum(inner, axis_two)
 
 
 def level_start(height):
@@ -135,8 +140,8 @@
         )
     else:
         slot_at = places[2] // 2**height
-        summed = lax.psum(
-            spread_slots(partial_value, total_span // 2**height, slot_at), ("gz", "row", "col")
+        summed = by_each_axis(
+            spread_slots(partial_value, total_span // 2**height, slot_at), ("row", "col"), "gz"
         )
     return lax.dynamic_index_in_dim(summed, slot_at, 0, keepdims=True)
 

time: 454 us -> 488 us (1.075)
  blocking collectives: 429 us -> 463 us
    psum x1 -> x2, blocking collectives: 41.4 us -> 79.4 us  [the longest x1 76 us: by_each_axis(): inner = lax.psum(value, axis_one)]
where the time goes in v1:
time: 488 us
  blocking collectives  463 us (95%)
  matrix products  9.61 us (2%)
  between operations  9.28 us (2%)
    psum x2, blocking collectives, group_total(): lax.psum(spread_slots(partial_value, grid_span // 2 ** height, slot_at),...  148 us
    psum x2, blocking collectives, group_share(): lax.psum(spread_slots(partial_value, grid_span // 2 ** height, slot_at),...  144 us
    psum x1, blocking collectives, by_each_axis(): inner = lax.psum(value, axis_one)  76 us
    psum x1, blocking collectives, group_total(): lax.psum(spread_slots(partial_value, total_span // 2 ** height, slot_at),...  36.9 us
    psum x2, blocking collectives, group_total(): lax.psum(spread_slots(partial_value, col_span // 2 ** height, slot_at).as...  29 us
    psum x2, blocking collectives, group_share(): lax.psum(spread_slots(partial_value, col_span // 2 ** height, slot_at).as...  25.9 us

profile of v1, /device:TPU:0, one launch (start us, length us, event | category | flops | bytes accessed | tf_op | source)
XLA Modules:
  0.0 487.5 jit_solution(6717787891907760853)
XLA Ops:
  0.0 0.7 compare_bitcast_fusion.3
  0.8 0.7 fusion.307
  1.5 1.1 convolution_multiply_fusion.1
  2.6 1.2 select_reduce_fusion.4
  3.9 1.4 convolution_multiply_fusion.13
  5.5 0.7 copy-done.5
  6.1 0.6 fusion.324
  10.2 20.5 %psum.77 = bf16[2,16,256]{2,1,0:T(8,128)(2,1)S(1)} all-reduce(bf16[2,16,256]{2,1,0:T(8,128)(2,1)S(1)} %select_convert_fusion.1), channel_id=1, replica_groups=mesh['gz'=2,'row'=4,'col'=4] {'col'}, use_global_device_ids=true, to_apply=%region_5.6 | all-reduce | flops 8192 | bytes 32768 | tf_op jit(solution)/shard_map/psum | solution.py:113
  30.7 0.7 copy-done.6
  31.4 0.6 dynamic_slice.24
  32.8 0.2 fusion.22
  35.9 8.5 %psum.78 = bf16[1,16,256]{2,1,0:T(8,128)(2,1)S(1)} all-reduce(bf16[1,16,256]{2,1,0:T(8,128)(2,1)S(1)} %fusion.218), channel_id=1, replica_groups=mesh['gz'=2,'row'=4,'col'=4] {'col'}, use_global_device_ids=true, to_apply=%region_6.7 | all-reduce | flops 4096 | bytes 16384 | tf_op jit(solution)/shard_map/psum | solution.py:113
  45.2 0.2 fusion.20
  45.8 75.8 %psum.79 = f32[2,16,256]{2,1,0:T(8,128)S(1)} all-reduce(f32[2,16,256]{2,1,0:T(8,128)S(1)} %broadcast_select_fusion.1), channel_id=1, replica_groups=mesh['gz'=2,'row'=4,'col'=4] {'row','col'}, use_global_device_ids=true, to_apply=%region_7.8 | all-reduce | flops 8192 | bytes 65536 | tf_op jit(solution)/shard_map/psum | solution.py:118
  122.6 0.2 fusion.18
  122.8 72.1 %psum.80 = f32[1,16,256]{2,1,0:T(8,128)S(1)} all-reduce(f32[1,16,256]{2,1,0:T(8,128)S(1)} %fusion.18), channel_id=1, replica_groups=mesh['gz'=2,'row'=4,'col'=4] {'row','col'}, use_global_device_ids=true, to_apply=%region_8.9 | all-reduce | flops 4096 | bytes 32768 | tf_op jit(solution)/shard_map/psum | solution.py:118
  195.7 0.2 fusion.13
  196.0 36.9 %psum.81 = f32[1,16,256]{2,1,0:T(8,128)S(1)} all-reduce(f32[1,16,256]{2,1,0:T(8,128)S(1)} %fusion.12), channel_id=1, replica_groups=mesh['gz'=2,'row'=4,'col'=4] {'gz','row','col'}, use_global_device_ids=true, to_apply=%region_9.10 | all-reduce | flops 4096 | bytes 32768 | tf_op jit(solution)/shard_map/psum | solution.py:123
  233.9 0.3 fusion.6
  234.3 76.0 %psum.82 = f32[1,16,256]{2,1,0:T(8,128)S(1)} all-reduce(f32[1,16,256]{2,1,0:T(8,128)S(1)} %select_bitcast_fusion.1), channel_id=1, replica_groups=mesh['gz'=2,'row'=4,'col'=4] {'row','col'}, use_global_device_ids=true, to_apply=%region_10.11 | all-reduce | flops 4096 | bytes 32768 | tf_op jit(solution)/shard_map/psum | solution.py:14
  310.3 3.3 psum.83
  313.8 0.3 fusion.5
  314.1 72.1 %psum.84 = f32[1,16,256]{2,1,0:T(8,128)S(1)} all-reduce(f32[1,16,256]{2,1,0:T(8,128)S(1)} %select_bitcast_fusion), channel_id=1, replica_groups=mesh['gz'=2,'row'=4,'col'=4] {'row','col'}, use_global_device_ids=true, to_apply=%region_12.13 | all-reduce | flops 4096 | bytes 32768 | tf_op jit(solution)/shard_map/psum | solution.py:138
  386.4 0.3 fusion.4
  386.8 72.1 %psum.85 = f32[2,16,256]{2,1,0:T(8,128)S(1)} all-reduce(f32[2,16,256]{2,1,0:T(8,128)S(1)} %broadcast_select_fusion), channel_id=1, replica_groups=mesh['gz'=2,'row'=4,'col'=4] {'row','col'}, use_global_device_ids=true, to_apply=%region_13.14 | all-reduce | flops 8192 | bytes 65536 | tf_op jit(solution)/shard_map/psum | solution.py:138
  459.1 0.3 fusion.3
  459.4 8.5 %psum.86 = bf16[1,16,256]{2,1,0:T(8,128)(2,1)S(1)} all-reduce(bf16[1,16,256]{2,1,0:T(8,128)(2,1)S(1)} %fusion.201), channel_id=1, replica_groups=mesh['gz'=2,'row'=4,'col'=4] {'col'}, use_global_device_ids=true, to_apply=%region_14.15 | all-reduce | flops 4096 | bytes 16384 | tf_op jit(solution)/shard_map/psum | solution.py:133
  468.1 0.3 fusion.2
  468.5 17.4 %psum.87 = bf16[2,16,256]{2,1,0:T(8,128)(2,1)S(1)} all-reduce(bf16[2,16,256]{2,1,0:T(8,128)(2,1)S(1)} %select_convert_fusion), channel_id=1, replica_groups=mesh['gz'=2,'row'=4,'col'=4] {'col'}, use_global_device_ids=true, to_apply=%region_15.16 | all-reduce | flops 8192 | bytes 32768 | tf_op jit(solution)/shard_map/psum | solution.py:133
  486.0 0.3 fusion.325
  486.6 0.3 fusion
  486.9 0.6 pad_maximum_fusion
  (66 shorter events, 3.5 us)
Async XLA Ops:
  0.0 5.3 %copy-start.1 = (bf16[1,4,2,256,256]{4,3,2,1,0:T(8,128)(2,1)S(1)}, bf16[1,4,2,256,256]{4,3,2,1,0:T(8,128)(2,1)}, u32[]{:S(2)}) copy-start(bf16[1,4,2,256,256]{4,3,2,1,0:T(8,128)(2,1)} %param.73) | copy-start | bytes 3145732
  3.9 28.8 %copy-start.2 = (bf16[1,4,256,256]{3,2,1,0:T(8,128)(2,1)S(1)}, bf16[1,4,256,256]{3,2,1,0:T(8,128)(2,1)}, u32[]{:S(2)}) copy-start(bf16[1,4,256,256]{3,2,1,0:T(8,128)(2,1)} %param.71) | copy-start | bytes 1572868
  5.5 0.7 copy-start.5
  10.1 22.6 %copy-start.4 = (f32[1,4,16,256]{3,2,1,0:T(8,128)S(1)}, f32[1,4,16,256]{3,2,1,0:T(8,128)}, u32[]{:S(2)}) copy-start(f32[1,4,16,256]{3,2,1,0:T(8,128)} %param.70) | copy-start | bytes 196612
  30.7 0.7 copy-start.6
  45.4 188.3 %copy-start = (bf16[1,4,2,256,256]{4,3,2,1,0:T(8,128)(2,1)S(1)}, bf16[1,4,2,256,256]{4,3,2,1,0:T(8,128)(2,1)}, u32[]{:S(2)}) copy-start(bf16[1,4,2,256,256]{4,3,2,1,0:T(8,128)(2,1)} %param.74) | copy-start | bytes 3145732
  195.5 38.4 %copy-start.3 = (bf16[1,4,256,256]{3,2,1,0:T(8,128)(2,1)S(1)}, bf16[1,4,256,256]{3,2,1,0:T(8,128)(2,1)}, u32[]{:S(2)}) copy-start(bf16[1,4,256,256]{3,2,1,0:T(8,128)(2,1)} %param.72) | copy-start | bytes 1572868
